TPU v7x, 128 devices: a whole 4x4x4 slice. The times are simulated.
128 devices in a mesh: row: 16 (over y, z), col: 8 (over x, core).
Axes of the slice: x: 4, y: 4, z: 4, core: 2. Of those that a mesh axis runs over, the one named last changes fastest.
Arguments:
- densities: bfloat16 [18432, 3072], P(('row', 'col')), may hold values from -0.796875 to 0.796875
- counts: int32 [2048], P(('row', 'col')), may hold values from 3 to 9
- coulomb: float32 [3072], replicated, may hold values from 0.05 to 1
- energies: float32 [18432], P(('row', 'col')), may hold values from 8 to 64
- vectors: bfloat16 [18432, 64], P(('row', 'col')), may hold values from -0.046875 to 0.046875
Outputs:
- kernel: float32 [18432, 18432], P('row', 'col')
- product: float32 [18432, 64], P(('row', 'col'))
All inputs are finite; a program needn't handle non-finite values.
Results may differ from a plain program's by a relative error of at most 0.0095.
Values may be sent and summed in bfloat16 or wider, within the bound.
No kernel may reach another device: no remote copies, remote signals or barrier semaphores. Data moves between devices by JAX's collectives and lax.ppermute only.
A program may use at most 128 MiB of HBM per device.

v0:
```python
import jax
import jax.numpy as jnp
from jax import lax
from jax.sharding import Mesh
from jax.sharding import PartitionSpec as P

SLOT = 9
ROW = ("row_0", "row_1")
ROW_COL = ("row_0", "row_1", "col")


def gather_axes(value, axes, dim):
    filled = value
    for number in range(len(axes) - 1, -1, -1):
        filled = lax.all_gather(filled, axes[number], axis=dim, tiled=True)
    return filled


def split_up(value, dim, count):
    before, after = (value.shape[:dim], value.shape[dim + 1 :])
    return jnp.moveaxis(value.reshape(*before, count, -1, *after), dim, 0)


def sent_and_summed(value, axis, dim):
    count = lax.axis_size(axis)
    blocks = lax.all_to_all(split_up(value, dim, count), axis, 0, 0, tiled=True)
    return jnp.sum(blocks.astype(jnp.float32), axis=0)


def split_product(matrix, right_side):
    high = matrix.astype(jnp.bfloat16)
    rest = matrix - high.astype(jnp.float32)
    middle = rest.astype(jnp.bfloat16)
    lowest = (rest - middle.astype(jnp.float32)).astype(jnp.bfloat16)
    total = jnp.dot(high, right_side, preferred_element_type=jnp.float32)
    total = total + jnp.dot(middle, right_side, preferred_element_type=jnp.float32)
    return total + jnp.dot(lowest, right_side, preferred_element_type=jnp.float32)


def body(densities, counts, coulomb, energies, vectors):
    kpoints = counts.shape[0]
    slot_index = lax.broadcasted_iota(jnp.int32, (kpoints, SLOT), 1)
    usable = (slot_index < counts[:, None]).reshape(kpoints * SLOT)
    masked = jnp.where(usable[:, None], densities, jnp.zeros_like(densities))
    weighted = (masked.astype(jnp.float32) * coulomb[None, :]).astype(jnp.bfloat16)
    row_block = lax.all_gather(weighted, "col", axis=0, tiled=True)
    kernel = lax.dot_general(
        row_block,
        lax.all_gather(masked, ROW, axis=0, tiled=True),
        (((1,), (1,)), ((), ())),
        preferred_element_type=jnp.float32,
    )
    column_vectors = gather_axes(vectors, ROW, 0)
    partial_value = split_product(kernel, column_vectors)
    coupled = sent_and_summed(partial_value.astype(jnp.bfloat16), "col", 0)
    diagonal = jnp.where(usable, energies, jnp.zeros_like(energies))
    product = coupled + diagonal[:, None] * vectors.astype(jnp.float32)
    return (kernel, product)


def solution(mesh):
    finer = Mesh(mesh.devices.reshape(4, 4, mesh.shape["col"]), ("row_0", "row_1", "col"))
    in_specs = (P(ROW_COL, None), P(ROW_COL), P(), P(ROW_COL), P(ROW_COL, None))
    out_specs = (P(ROW, "col"), P(ROW_COL, None))
    return jax.shard_map(body, mesh=finer, in_specs=in_specs, out_specs=out_specs, check_vma=False)
```

profile of v0, /device:TPU:1, one launch (start us, length us, event | category | flops | bytes accessed | tf_op | source)
XLA Modules:
  0.0 206.2 jit_solution(9412224943959909971)
XLA Ops:
  7.2 0.0 all-gather.5.cloned.1.call-start
  7.2 0.7 iota_compare_fusion
  7.9 0.1 lt.18
  8.0 2.8 %multiply_convert_fusion = (bf16[144,3072]{1,0:T(8,128)(2,1)}, bf16[144,3072]{1,0:T(8,128)(2,1)}) fusion(f32[3072]{0:T(1024)} %param.7, bf16[144,3072]{1,0:T(8,128)(2,1)} %param.5, pred[144]{0:T(512)(128)(4,1)S(1)} %lt.18), kind=kLoop, calls=%fused_computation.10 | loop fusion | flops 1769472 | bytes 2666640 | tf_op jit(solution)/shard_map/convert_element_type | solution.py:45
  10.8 0.0 all-gather.5.cloned.1.call-update
  10.8 0.0 all-gather.7.cloned.1.call-start
  10.9 0.7 all-gather.7.cloned.1.call-update
  11.6 11.8 %all-gather = bf16[4,144,64]{1,2,0:T(8,128)(2,1)S(1)} all-gather(bf16[1,144,64]{1,2,0:T(8,128)(2,1)} %bitcast.12), channel_id=1, replica_groups=mesh['row_0'=4,'row_1'=4,'col'=8] {'row_1'}, dimensions={0}, use_global_device_ids=true | all-gather | bytes 92160 | tf_op jit(solution)/shard_map/all_gather | solution.py:15
  23.4 0.1 copy.10
  23.5 0.1 reshape.30
  23.6 11.2 %all-gather.1 = bf16[4,576,64]{1,2,0:T(8,128)(2,1)S(1)} all-gather(bf16[1,576,64]{1,2,0:T(8,128)(2,1)S(1)} %reshape.30), channel_id=1, replica_groups=mesh['row_0'=4,'row_1'=4,'col'=8] {'row_0'}, dimensions={0}, use_global_device_ids=true | all-gather | bytes 368640 | tf_op jit(solution)/shard_map/all_gather | solution.py:15
  34.9 0.3 copy.11
  35.1 0.3 reshape.31
  35.4 23.3 %all-gather.5.cloned.1.call-done = bf16[1152,3072]{1,0:T(8,128)(2,1)} async-done(((bf16[144,3072]{1,0:T(8,128)(2,1)}), bf16[1152,3072]{1,0:T(8,128)(2,1)}) %all-gather.5.cloned.1.call-update) | async-done | bytes 7077904 | tf_op jit(solution)/shard_map/all_gather | solution.py:46
  58.7 99.7 %all-gather.7.cloned.1.call-done = bf16[2304,3072]{1,0:T(8,128)(2,1)} async-done(((bf16[144,3072]{1,0:T(8,128)(2,1)}), bf16[2304,3072]{1,0:T(8,128)(2,1)}) %all-gather.7.cloned.1.call-update) | async-done | bytes 14155792 | tf_op jit(solution)/shard_map/all_gather | solution.py:49
  158.4 21.7 %fusion.11 = f32[1152,2304]{1,0:T(8,128)S(1)} fusion(bf16[1152,3072]{1,0:T(8,128)(2,1)} %all-gather.5.cloned.1.call-done, bf16[2304,3072]{1,0:T(8,128)(2,1)} %all-gather.7.cloned.1.call-done), kind=kOutput, calls=%fused_computation.16 | convolution fusion | flops 16307453952 | bytes 31850496 | tf_op jit(solution)/shard_map/dot_general | solution.py:47
  180.1 0.0 copy-start
  180.1 1.7 fusion.1
  181.9 1.8 fusion.7
  183.6 0.6 copy-done
  184.2 0.0 copy-start.2
  184.2 0.0 copy-start.1
  184.2 1.8 fusion.10
  186.0 0.4 reshape.27
  186.4 0.7 copy.12
  187.1 5.1 %all-to-all-start = ((bf16[8,144,64]{1,2,0:T(8,128)(2,1)}), bf16[8,144,64]{1,2,0:T(8,128)(2,1)S(1)}, u32[]{:S(2)}, u32[]{:S(2)}) async-start(bf16[8,144,64]{1,2,0:T(8,128)(2,1)} %copy.12), calls=%async_computation | async-start | bytes 524288 | tf_op jit(solution)/shard_map/all_to_all | solution.py:26
  192.2 0.0 copy-done.2
  192.2 6.5 %all-to-all-done = bf16[8,144,64]{1,2,0:T(8,128)(2,1)S(1)} async-done(((bf16[8,144,64]{1,2,0:T(8,128)(2,1)}), bf16[8,144,64]{1,2,0:T(8,128)(2,1)S(1)}, u32[]{:S(2)}, u32[]{:S(2)}) %all-to-all-start) | async-done | bytes 147488 | tf_op jit(solution)/shard_map/all_to_all | solution.py:26
  198.8 0.0 copy-done.1
  198.8 0.6 multiply_add_fusion
  (2 shorter events, 0.1 us)
Async XLA Ops:
  7.2 51.6 %all-gather.5.cloned.1.call-start = ((), (), s32[]{:S(2)}) async-start(), calls=%async_computation.1 | async-start | bytes 7962624 | tf_op jit(solution)/shard_map/all_gather | solution.py:46
  10.8 147.6 %all-gather.7.cloned.1.call-start = ((), (), s32[]{:S(2)}) async-start(), calls=%async_computation.2 | async-start | bytes 15040512 | tf_op jit(solution)/shard_map/all_gather | solution.py:49
  180.1 4.1 %copy-start = (f32[1152,2304]{1,0:T(8,128)}, f32[1152,2304]{1,0:T(8,128)S(1)}, u32[]{:S(2)}) copy-start(f32[1152,2304]{1,0:T(8,128)S(1)} %fusion.11) | copy-start | bytes 31850500
  184.2 8.0 %copy-start.2 = (f32[144]{0:T(256)S(1)}, f32[144]{0:T(256)}, u32[]{:S(2)}) copy-start(f32[144]{0:T(256)} %param.8) | copy-start | bytes 1732
  184.2 14.5 %copy-start.1 = (bf16[144,64]{0,1:T(8,128)(2,1)S(1)}, bf16[144,64]{0,1:T(8,128)(2,1)}, u32[]{:S(2)}) copy-start(bf16[144,64]{0,1:T(8,128)(2,1)} %param.9) | copy-start | bytes 55300
  187.1 11.6 %all-to-all-start = ((bf16[8,144,64]{1,2,0:T(8,128)(2,1)}), bf16[8,144,64]{1,2,0:T(8,128)(2,1)S(1)}, u32[]{:S(2)}, u32[]{:S(2)}) async-start(bf16[8,144,64]{1,2,0:T(8,128)(2,1)} %copy.12), calls=%async_computation | async-start | bytes 524288 | tf_op jit(solution)/shard_map/all_to_all | solution.py:26
Sparse Core Ops, SparseCore 0:
  11.0 47.7 all-gather.4
  60.9 97.4 all-gather.6
where the time goes:
time: 207 us; the launch traced here: 206 us
  waiting for transfers between devices  130 us (63%)
  matrix products  27 us (13%)
  blocking collectives  23 us (11%)
  between operations  14.1 us (7%)
  starting transfers between devices  5.17 us (2%)
  other arithmetic  4.2 us (2%)
  local copies, waits for them, and re-layouts  2.6 us (1%)
    all_gather x1, waiting for transfers between devices, body(): lax.all_gather(masked, ROW, axis=0, tiled=True)  99.7 us
    all_gather x1, waiting for transfers between devices, body(): row_block = lax.all_gather(weighted, 'col', axis=0, tiled=True)  23.3 us
    all_gather x2, blocking collectives, gather_axes(): filled = lax.all_gather(filled, axes[number], axis=dim, tiled=True)  23 us
    dot_general x1, matrix products, body(): lax.dot_general(row_block, lax.all_gather(masked, ROW, axis=0, tiled=True...  21.7 us
    all_to_all x1, waiting for transfers between devices, sent_and_summed(): blocks = lax.all_to_all(split_up(value, dim, count), axis, 0, 0, tiled=True)  6.46 us
    all_to_all x1, starting transfers between devices, sent_and_summed(): blocks = lax.all_to_all(split_up(value, dim, count), axis, 0, 0, tiled=True)  5.09 us
  transfers between devices with their start and end apart: 3, of which 3 were waited for; matrix products, arithmetic and copies ran while one was open for 0% of the time, Pallas kernels for 0%

commit v1 on v0

--- a/solution.py
+++ b/solution.py
@@ -7,6 +7,27 @@
 SLOT = 9
 ROW = ("row_0", "row_1")
 ROW_COL = ("row_0", "row_1", "col")
+
+
+def collect(value, axis, dim):
+    size, here, extent = (lax.axis_size(axis), lax.axis_index(axis), value.shape[dim])
+    right = [(i, (i + 1) % size) for i in range(size)]
+    left = [(i, (i - 1) % size) for i in range(size)]
+    whole = jnp.zeros((*value.shape[:dim], size * extent, *value.shape[dim + 1 :]), value.dtype)
+    whole = lax.dynamic_update_slice_in_dim(whole, value, here * extent, axis=dim)
+    from_left = from_right = value
+    half = size // 2
+    for step in range(1, half + 1):
+        from_left = lax.ppermute(from_left, axis, right)
+        whole = lax.dynamic_update_slice_in_dim(
+            whole, from_left, (here - step) % size * extent, axis=dim
+        )
+        if step < size - half:
+            from_right = lax.ppermute(from_right, axis, left)
+            whole = lax.dynamic_update_slice_in_dim(
+                whole, from_right, (here + step) % size * extent, axis=dim
+            )
+    return whole
 
 
 def gather_axes(value, axes, dim):
@@ -43,7 +64,7 @@
     usable = (slot_index < counts[:, None]).reshape(kpoints * SLOT)
     masked = jnp.where(usable[:, None], densities, jnp.zeros_like(densities))
     weighted = (masked.astype(jnp.float32) * coulomb[None, :]).astype(jnp.bfloat16)
-    row_block = lax.all_gather(weighted, "col", axis=0, tiled=True)
+    row_block = collect(weighted, "col", 0)
     kernel = lax.dot_general(
         row_block,
         lax.all_gather(masked, ROW, axis=0, tiled=True),

time: 207 us -> 164 us (0.79)
  waiting for transfers between devices: 130 us -> 61.8 us
  starting transfers between devices: 5.17 us -> 19.6 us
  local copies, waits for them, and re-layouts: 2.6 us -> 14.4 us
    all_gather x1, waiting for transfers between devices: 99.7 us -> 33.7 us  [body(): lax.all_gather(masked, ROW, axis=0, tiled=True)]
    all_gather x1 -> x0, waiting for transfers between devices: 23.3 us -> none  [body(): row_block = lax.all_gather(weighted, 'col', axis=0, tiled=True)]
    ppermute x0 -> x7, waiting for transfers between devices: none -> 21.6 us  [the longest x4 20.1 us: collect(): from_left = lax.ppermute(from_left, axis, right)]
    ppermute x0 -> x7, starting transfers between devices: none -> 14.8 us  [the longest x4 13.4 us: collect(): from_left = lax.ppermute(from_left, axis, right)]
    dynamic_update_slice x0 -> x7, local copies, waits for them, and re-layouts: none -> 7.94 us  [the longest x4 5.04 us: collect(): lax.dynamic_update_slice_in_dim(whole, from_left, (here - step) % size *...]
    broadcast_in_dim x0 -> x1, local copies, waits for them, and re-layouts: none -> 3.85 us  [collect(): jnp.zeros((*value.shape[:dim], size * extent, *value.shape[dim + 1:]), va...]
    convert_element_type x1 -> x0, other arithmetic: 2.78 us -> none  [body(): (masked.astype(jnp.float32) * coulomb[None, :]).astype(jnp.bfloat16)]
  transfers between devices with their start and end apart: 3 -> 9, of which waited for: 3 -> 6; matrix products, arithmetic and copies ran while one was open for 0% -> 5% of each run, Pallas kernels for 0% -> 0%
where the time goes in v1:
time: 164 us
  waiting for transfers between devices  61.8 us (38%)
  matrix products  27 us (16%)
  blocking collectives  23.6 us (14%)
  starting transfers between devices  19.6 us (12%)
  local copies, waits for them, and re-layouts  14.4 us (9%)
  between operations  14.2 us (9%)
  other arithmetic  3.16 us (2%)
    all_gather x1, waiting for transfers between devices, body(): lax.all_gather(masked, ROW, axis=0, tiled=True)  33.7 us
    all_gather x2, blocking collectives, gather_axes(): filled = lax.all_gather(filled, axes[number], axis=dim, tiled=True)  23.6 us
    dot_general x1, matrix products, body(): lax.dot_general(row_block, lax.all_gather(masked, ROW, axis=0, tiled=True...  21.7 us
    ppermute x4, waiting for transfers between devices, collect(): from_left = lax.ppermute(from_left, axis, right)  20.1 us
    ppermute x4, starting transfers between devices, collect(): from_left = lax.ppermute(from_left, axis, right)  13.4 us
    all_to_all x1, waiting for transfers between devices, sent_and_summed(): blocks = lax.all_to_all(split_up(value, dim, count), axis, 0, 0, tiled=True)  6.46 us
    dynamic_update_slice x4, local copies, waits for them, and re-layouts, collect(): lax.dynamic_update_slice_in_dim(whole, from_left, (here - step) % size *...  5.04 us
    all_to_all x1, starting transfers between devices, sent_and_summed(): blocks = lax.all_to_all(split_up(value, dim, count), axis, 0, 0, tiled=True)  4.75 us
  transfers between devices with their start and end apart: 9, of which 6 were waited for; matrix products, arithmetic and copies ran while one was open for 5% of the time, Pallas kernels for 0%

profile of v1, /device:TPU:1, one launch (start us, length us, event | category | flops | bytes accessed | tf_op | source)
XLA Modules:
  0.0 163.7 jit_solution(17550822412426189017)
XLA Ops:
  7.2 0.0 copy-start.1
  7.2 0.0 copy-start.3
  7.2 0.0 copy-start.2
  7.2 0.0 all-gather.4.cloned.1.call-start
  7.2 0.8 iota_compare_fusion
  8.0 0.1 lt.72
  8.1 3.9 %broadcast_in_dim.20 = bf16[1152,3072]{1,0:T(8,128)(2,1)} broadcast(bf16[]{:T(256)} %constant.52.clone.1), dimensions={} | broadcast | bytes 7077890 | tf_op jit(solution)/shard_map/broadcast_in_dim | solution.py:16
  12.0 0.0 copy-done.1
  12.0 0.0 copy-done.3
  12.0 1.7 %constant_dynamic-update-slice_fusion.7 = (bf16[1152,3072]{1,0:T(8,128)(2,1)}, bf16[144,3072]{1,0:T(8,128)(2,1)S(1)}, bf16[144,3072]{1,0:T(8,128)(2,1)}) fusion(bf16[1152,3072]{1,0:T(8,128)(2,1)} %broadcast_in_dim.20, s32[]{:T(128)S(6)} %select_n.64, f32[3072]{0:T(1024)S(1)} %copy-done.3, bf16[144,3072]{1,0:T(8,128)(2,1)S(1)} %copy-done.1, ...), kind=kLoop, calls=%fused_computation.22 | loop fusion | flops 1769472 | bytes 3551380 | tf_op jit(solution)/shard_map/dynamic_update_slice | solution.py:17
  13.7 0.0 all-gather.4.cloned.1.call-update
  13.7 2.6 %collective-permute-start = (bf16[144,3072]{1,0:T(8,128)(2,1)S(1)}, bf16[144,3072]{1,0:T(8,128)(2,1)}, u32[]{:S(2)}, u32[]{:S(2)}) collective-permute-start(bf16[144,3072]{1,0:T(8,128)(2,1)S(1)} %get-tuple-element.3), channel_id=1, source_target_pairs={{0,1},{1,2},{2,3},{3,4},{4,5},{5,6},{6,7},{7,0},{8,9},{9,10},{10,1... | collective-permute-start | bytes 2654216 | tf_op jit(solution)/shard_map/ppermute | solution.py:21
  16.3 0.0 collective-permute-start.1
  16.3 10.0 %collective-permute-done = bf16[144,3072]{1,0:T(8,128)(2,1)} collective-permute-done((bf16[144,3072]{1,0:T(8,128)(2,1)S(1)}, bf16[144,3072]{1,0:T(8,128)(2,1)}, u32[]{:S(2)}, u32[]{:S(2)}) %collective-permute-start) | collective-permute-done | bytes 884768 | tf_op jit(solution)/shard_map/ppermute | solution.py:21
  26.3 2.6 %collective-permute-start.2 = (bf16[144,3072]{1,0:T(8,128)(2,1)}, bf16[144,3072]{1,0:T(8,128)(2,1)S(1)}, u32[]{:S(2)}, u32[]{:S(2)}) collective-permute-start(bf16[144,3072]{1,0:T(8,128)(2,1)} %collective-permute-done), channel_id=1, source_target_pairs={{0,1},{1,2},{2,3},{3,4},{4,5},{5,6},{6,7},{7,0},{8,9},{9,10},{10,1... | collective-permute-start | bytes 2654216 | tf_op jit(solution)/shard_map/ppermute | solution.py:21
  28.9 0.0 collective-permute-done.1
  28.9 0.0 collective-permute-start.3
  28.9 0.0 copy-done.2
  28.9 12.3 %all-gather = bf16[4,144,64]{1,2,0:T(8,128)(2,1)S(1)} all-gather(bf16[1,144,64]{1,2,0:T(8,128)(2,1)S(1)} %bitcast.12), channel_id=1, replica_groups=mesh['row_0'=4,'row_1'=4,'col'=8] {'row_1'}, dimensions={0}, use_global_device_ids=true | all-gather | bytes 92160 | tf_op jit(solution)/shard_map/all_gather | solution.py:36
  41.2 0.1 copy.10
  41.3 0.1 reshape.30
  41.4 11.3 %all-gather.1 = bf16[4,576,64]{1,2,0:T(8,128)(2,1)S(1)} all-gather(bf16[1,576,64]{1,2,0:T(8,128)(2,1)S(1)} %reshape.30), channel_id=1, replica_groups=mesh['row_0'=4,'row_1'=4,'col'=8] {'row_0'}, dimensions={0}, use_global_device_ids=true | all-gather | bytes 368640 | tf_op jit(solution)/shard_map/all_gather | solution.py:36
  52.7 0.3 copy.11
  53.0 0.3 reshape.31
  53.3 0.0 collective-permute-done.2
  53.3 5.8 %collective-permute-start.4 = (bf16[144,3072]{1,0:T(8,128)(2,1)S(1)}, bf16[144,3072]{1,0:T(8,128)(2,1)S(1)}, u32[]{:S(2)}, u32[]{:S(2)}) collective-permute-start(bf16[144,3072]{1,0:T(8,128)(2,1)S(1)} %collective-permute-done.2), channel_id=1, source_target_pairs={{0,1},{1,2},{2,3},{3,4},{4,5},{5,6},{6,7},{7,0},{8,9},{9,10},{10,1... | collective-permute-start | bytes 2654216 | tf_op jit(solution)/shard_map/ppermute | solution.py:21
  59.1 2.1 %constant_dynamic-update-slice_fusion.6 = bf16[1152,3072]{1,0:T(8,128)(2,1)} fusion(bf16[1152,3072]{1,0:T(8,128)(2,1)} %get-tuple-element.2, bf16[144,3072]{1,0:T(8,128)(2,1)} %collective-permute-done, s32[]{:T(128)S(6)} %select_n.66), kind=kLoop, calls=%fused_computation.21 | loop fusion | bytes 1769476 | tf_op jit(solution)/shard_map/dynamic_update_slice | solution.py:22
  61.2 1.0 constant_dynamic-update-slice_fusion.5
  62.2 0.0 collective-permute-done.3
  62.2 1.4 collective-permute-start.5
  63.6 1.0 constant_dynamic-update-slice_fusion.4
  64.5 4.6 %collective-permute-done.4 = bf16[144,3072]{1,0:T(8,128)(2,1)S(1)} collective-permute-done((bf16[144,3072]{1,0:T(8,128)(2,1)S(1)}, bf16[144,3072]{1,0:T(8,128)(2,1)S(1)}, u32[]{:S(2)}, u32[]{:S(2)}) %collective-permute-start.4) | collective-permute-done | bytes 884768 | tf_op jit(solution)/shard_map/ppermute | solution.py:21
  69.1 2.5 %collective-permute-start.6 = (bf16[144,3072]{1,0:T(8,128)(2,1)S(1)}, bf16[144,3072]{1,0:T(8,128)(2,1)S(1)}, u32[]{:S(2)}, u32[]{:S(2)}) collective-permute-start(bf16[144,3072]{1,0:T(8,128)(2,1)S(1)} %collective-permute-done.4), channel_id=1, source_target_pairs={{0,1},{1,2},{2,3},{3,4},{4,5},{5,6},{6,7},{7,0},{8,9},{9,10},{10,1... | collective-permute-start | bytes 2654216 | tf_op jit(solution)/shard_map/ppermute | solution.py:21
  71.6 1.0 constant_dynamic-update-slice_fusion.3
  72.5 1.0 constant_dynamic-update-slice_fusion.2
  73.5 1.6 collective-permute-done.5
  75.1 1.0 constant_dynamic-update-slice_fusion.1
  76.0 5.5 %collective-permute-done.6 = bf16[144,3072]{1,0:T(8,128)(2,1)S(1)} collective-permute-done((bf16[144,3072]{1,0:T(8,128)(2,1)S(1)}, bf16[144,3072]{1,0:T(8,128)(2,1)S(1)}, u32[]{:S(2)}, u32[]{:S(2)}) %collective-permute-start.6) | collective-permute-done | bytes 884768 | tf_op jit(solution)/shard_map/ppermute | solution.py:21
  81.6 1.0 constant_dynamic-update-slice_fusion
  82.5 33.7 %all-gather.4.cloned.1.call-done = bf16[2304,3072]{1,0:T(8,128)(2,1)} async-done(((bf16[144,3072]{1,0:T(8,128)(2,1)}), bf16[2304,3072]{1,0:T(8,128)(2,1)}) %all-gather.4.cloned.1.call-update) | async-done | bytes 14155792 | tf_op jit(solution)/shard_map/all_gather | solution.py:70
  116.2 21.7 %fusion.11 = f32[1152,2304]{1,0:T(8,128)S(1)} fusion(bf16[1152,3072]{1,0:T(8,128)(2,1)} %constant_dynamic-update-slice_fusion, bf16[2304,3072]{1,0:T(8,128)(2,1)} %all-gather.4.cloned.1.call-done), kind=kOutput, calls=%fused_computation.24 | convolution fusion | flops 16307453952 | bytes 31850496 | tf_op jit(solution)/shard_map/dot_general | solution.py:68
  137.9 0.0 copy-start
  137.9 1.7 %fusion.1 = f32[1152,64]{0,1:T(8,128)S(1)} fusion(bf16[2304,64]{0,1:T(8,128)(2,1)S(1)} %reshape.31, f32[1152,2304]{1,0:T(8,128)S(1)} %fusion.11), kind=kOutput, calls=%fused_computation.3 | convolution fusion | flops 342392832 | bytes 11206656 | tf_op jit(solution)/shard_map/dot_general | solution.py:56
  139.6 1.8 %fusion.7 = f32[1152,64]{0,1:T(8,128)S(1)} fusion(f32[1152,64]{0,1:T(8,128)S(1)} %fusion.1, bf16[2304,64]{0,1:T(8,128)(2,1)S(1)} %reshape.31, f32[1152,2304]{1,0:T(8,128)S(1)} %fusion.11), kind=kOutput, calls=%fused_computation.8 | convolution fusion | flops 350429184 | bytes 11501568 | tf_op jit(solution)/shard_map/dot_general | solution.py:57
  141.4 0.6 copy-done
  142.0 0.0 copy-start.4
  142.0 1.8 %fusion.10 = bf16[1152,64]{0,1:T(8,128)(2,1)S(1)} fusion(f32[1152,64]{0,1:T(8,128)S(1)} %fusion.7, bf16[2304,64]{0,1:T(8,128)(2,1)S(1)} %reshape.31, f32[1152,2304]{1,0:T(8,128)S(1)} %fusion.11), kind=kOutput, calls=%fused_computation.9 | convolution fusion | flops 358465536 | bytes 11354112 | tf_op jit(solution)/shard_map/dot_general | solution.py:58
  143.8 0.4 reshape.27
  144.2 0.7 copy.12
  144.9 4.8 %all-to-all-start = ((bf16[8,144,64]{1,2,0:T(8,128)(2,1)}), bf16[8,144,64]{1,2,0:T(8,128)(2,1)S(1)}, u32[]{:S(2)}, u32[]{:S(2)}) async-start(bf16[8,144,64]{1,2,0:T(8,128)(2,1)} %copy.12), calls=%async_computation | async-start | bytes 524288 | tf_op jit(solution)/shard_map/all_to_all | solution.py:47
  149.7 0.0 copy-done.4
  149.7 6.5 %all-to-all-done = bf16[8,144,64]{1,2,0:T(8,128)(2,1)S(1)} async-done(((bf16[8,144,64]{1,2,0:T(8,128)(2,1)}), bf16[8,144,64]{1,2,0:T(8,128)(2,1)S(1)}, u32[]{:S(2)}, u32[]{:S(2)}) %all-to-all-start) | async-done | bytes 147488 | tf_op jit(solution)/shard_map/all_to_all | solution.py:47
  156.2 0.6 multiply_add_fusion
  (2 shorter events, 0.1 us)
Async XLA Ops:
  7.2 4.8 %copy-start.1 = (bf16[144,3072]{1,0:T(8,128)(2,1)S(1)}, bf16[144,3072]{1,0:T(8,128)(2,1)}, u32[]{:S(2)}) copy-start(bf16[144,3072]{1,0:T(8,128)(2,1)} %param.5) | copy-start | bytes 2654212
  7.2 4.8 %copy-start.3 = (f32[3072]{0:T(1024)S(1)}, f32[3072]{0:T(1024)}, u32[]{:S(2)}) copy-start(f32[3072]{0:T(1024)} %param.7) | copy-start | bytes 36868
  7.2 21.7 %copy-start.2 = (bf16[144,64]{0,1:T(8,128)(2,1)S(1)}, bf16[144,64]{0,1:T(8,128)(2,1)}, u32[]{:S(2)}) copy-start(bf16[144,64]{0,1:T(8,128)(2,1)} %param.9) | copy-start | bytes 55300
  7.2 109.0 %all-gather.4.cloned.1.call-start = ((), (), s32[]{:S(2)}) async-start(), calls=%async_computation.1 | async-start | bytes 15040512 | tf_op jit(solution)/shard_map/all_gather | solution.py:70
  13.7 12.6 %collective-permute-start = (bf16[144,3072]{1,0:T(8,128)(2,1)S(1)}, bf16[144,3072]{1,0:T(8,128)(2,1)}, u32[]{:S(2)}, u32[]{:S(2)}) collective-permute-start(bf16[144,3072]{1,0:T(8,128)(2,1)S(1)} %get-tuple-element.3), channel_id=1, source_target_pairs={{0,1},{1,2},{2,3},{3,4},{4,5},{5,6},{6,7},{7,0},{8,9},{9,10},{10,1... | collective-permute-start | bytes 2654216 | tf_op jit(solution)/shard_map/ppermute | solution.py:21
  16.3 12.6 %collective-permute-start.1 = (bf16[144,3072]{1,0:T(8,128)(2,1)S(1)}, bf16[144,3072]{1,0:T(8,128)(2,1)S(1)}, u32[]{:S(2)}, u32[]{:S(2)}) collective-permute-start(bf16[144,3072]{1,0:T(8,128)(2,1)S(1)} %get-tuple-element.3), channel_id=1, source_target_pairs={{0,7},{1,0},{2,1},{3,2},{4,3},{5,4},{6,5},{7,6},{8,15},{9,8},{10,9... | collective-permute-start | bytes 2654216 | tf_op jit(solution)/shard_map/ppermute | solution.py:26
  26.3 27.0 %collective-permute-start.2 = (bf16[144,3072]{1,0:T(8,128)(2,1)}, bf16[144,3072]{1,0:T(8,128)(2,1)S(1)}, u32[]{:S(2)}, u32[]{:S(2)}) collective-permute-start(bf16[144,3072]{1,0:T(8,128)(2,1)} %collective-permute-done), channel_id=1, source_target_pairs={{0,1},{1,2},{2,3},{3,4},{4,5},{5,6},{6,7},{7,0},{8,9},{9,10},{10,1... | collective-permute-start | bytes 2654216 | tf_op jit(solution)/shard_map/ppermute | solution.py:21
  28.9 33.3 %collective-permute-start.3 = (bf16[144,3072]{1,0:T(8,128)(2,1)S(1)}, bf16[144,3072]{1,0:T(8,128)(2,1)S(1)}, u32[]{:S(2)}, u32[]{:S(2)}) collective-permute-start(bf16[144,3072]{1,0:T(8,128)(2,1)S(1)} %collective-permute-done.1), channel_id=1, source_target_pairs={{0,7},{1,0},{2,1},{3,2},{4,3},{5,4},{6,5},{7,6},{8,15},{9,8},{10,9... | collective-permute-start | bytes 2654216 | tf_op jit(solution)/shard_map/ppermute | solution.py:26
  53.3 15.8 %collective-permute-start.4 = (bf16[144,3072]{1,0:T(8,128)(2,1)S(1)}, bf16[144,3072]{1,0:T(8,128)(2,1)S(1)}, u32[]{:S(2)}, u32[]{:S(2)}) collective-permute-start(bf16[144,3072]{1,0:T(8,128)(2,1)S(1)} %collective-permute-done.2), channel_id=1, source_target_pairs={{0,1},{1,2},{2,3},{3,4},{4,5},{5,6},{6,7},{7,0},{8,9},{9,10},{10,1... | collective-permute-start | bytes 2654216 | tf_op jit(solution)/shard_map/ppermute | solution.py:21
  62.2 12.9 %collective-permute-start.5 = (bf16[144,3072]{1,0:T(8,128)(2,1)S(1)}, bf16[144,3072]{1,0:T(8,128)(2,1)S(1)}, u32[]{:S(2)}, u32[]{:S(2)}) collective-permute-start(bf16[144,3072]{1,0:T(8,128)(2,1)S(1)} %collective-permute-done.3), channel_id=1, source_target_pairs={{0,7},{1,0},{2,1},{3,2},{4,3},{5,4},{6,5},{7,6},{8,15},{9,8},{10,9... | collective-permute-start | bytes 2654216 | tf_op jit(solution)/shard_map/ppermute | solution.py:26
  69.1 12.5 %collective-permute-start.6 = (bf16[144,3072]{1,0:T(8,128)(2,1)S(1)}, bf16[144,3072]{1,0:T(8,128)(2,1)S(1)}, u32[]{:S(2)}, u32[]{:S(2)}) collective-permute-start(bf16[144,3072]{1,0:T(8,128)(2,1)S(1)} %collective-permute-done.4), channel_id=1, source_target_pairs={{0,1},{1,2},{2,3},{3,4},{4,5},{5,6},{6,7},{7,0},{8,9},{9,10},{10,1... | collective-permute-start | bytes 2654216 | tf_op jit(solution)/shard_map/ppermute | solution.py:21
  137.9 4.1 %copy-start = (f32[1152,2304]{1,0:T(8,128)}, f32[1152,2304]{1,0:T(8,128)S(1)}, u32[]{:S(2)}) copy-start(f32[1152,2304]{1,0:T(8,128)S(1)} %fusion.11) | copy-start | bytes 31850500
  142.0 7.7 %copy-start.4 = (f32[144]{0:T(256)S(1)}, f32[144]{0:T(256)}, u32[]{:S(2)}) copy-start(f32[144]{0:T(256)} %param.8) | copy-start | bytes 1732
  144.9 11.2 %all-to-all-start = ((bf16[8,144,64]{1,2,0:T(8,128)(2,1)}), bf16[8,144,64]{1,2,0:T(8,128)(2,1)S(1)}, u32[]{:S(2)}, u32[]{:S(2)}) async-start(bf16[8,144,64]{1,2,0:T(8,128)(2,1)} %copy.12), calls=%async_computation | async-start | bytes 524288 | tf_op jit(solution)/shard_map/all_to_all | solution.py:47
Sparse Core Ops, SparseCore 0:
  13.8 102.3 all-gather.3
